TPU v7x, 32 devices: a whole 2x2x4 slice. The times are simulated.
32 devices in a mesh: pair: 4 (over y, x), aux: 8 (over z, core).
Axes of the slice: x: 2, y: 2, z: 4, core: 2. Of those that a mesh axis runs over, the one named last changes fastest.
Arguments:
- amplitudes: bfloat16 [4, 512, 512], P('pair', 'aux'), may hold values from -6 to 6
- factors: bfloat16 [4096, 512, 512], P('aux', 'pair'), may hold values from -0.03125 to 0.03125
- hole_weights: float32 [4, 4], replicated, may hold values from -3 to 3
- driver: float32 [4, 6, 512], P('pair', None, 'aux'), may hold values from -6 to 6
- eps_vir: float32 [512], replicated, may hold values from 0.5 to 3
- pair_energy: float32 [4], P('pair'), may hold values from -3 to -0.5
Outputs:
- residual: float32 [4, 6, 512], P('pair', None, 'aux')
- new_amps: float32 [4, 6, 512], P('pair', None, 'aux')
All inputs are finite; a program needn't handle non-finite values.
Results may differ from a plain program's by a relative error of at most 0.0003.
Values may be sent and summed in bfloat16 or wider, within the bound.
A program may use at most 192 MiB of HBM per device.

v0:
```python
import jax
import jax.numpy as jnp
from jax import lax
from jax.sharding import PartitionSpec as P


def broadcast(block, axis, source):
    block = jnp.where(lax.axis_index(axis) == source, block, jnp.zeros_like(block))
    return lax.psum(block, axis)


def half_of(window, amp_pair):
    return jnp.einsum("qac,cd->aqd", window, amp_pair, preferred_element_type=jnp.float32).astype(
        jnp.bfloat16
    )


def contract(halves, factors):
    return jnp.einsum("aqd,qbd->ab", halves, factors, preferred_element_type=jnp.float32)


def per_device(amplitudes, factors, hole_weights, driver, eps_vir, pair_energy):
    window_rows = driver.shape[1]
    columns = driver.shape[2]
    amp_full = lax.all_gather(amplitudes, "aux", axis=1, tiled=True)
    window = broadcast(factors[:, :window_rows, :], "pair", 0)
    amp_window = amp_full[:, :window_rows, :]
    slab = lax.all_to_all(amp_window, "pair", split_axis=2, concat_axis=0, tiled=True)

    def ladder_pair(amp_pair):
        return contract(half_of(window, amp_pair), factors)

    particle = lax.map(ladder_pair, lax.all_gather(amp_full, "pair", axis=0, tiled=True))
    hole_term = jnp.einsum(
        "pk,kab->pab", hole_weights, slab.astype(jnp.float32), precision=lax.Precision.HIGHEST
    )
    aux_index = lax.axis_index("aux")
    partial_value = particle + jnp.where(aux_index == 0, hole_term, 0.0)
    returned = lax.all_to_all(partial_value, "pair", split_axis=0, concat_axis=2, tiled=True)
    summed = lax.psum_scatter(returned, "aux", scatter_dimension=2, tiled=True)
    residual = driver + summed
    column_start = aux_index * columns
    amp_cols = lax.dynamic_slice_in_dim(amp_window, column_start, columns, 2).astype(jnp.float32)
    eps_cols = lax.dynamic_slice_in_dim(eps_vir, column_start, columns, 0)
    denominator = (
        eps_vir[:window_rows][None, :, None] + eps_cols[None, None, :] - pair_energy[:, None, None]
    )
    new_amps = amp_cols - residual / denominator
    return (residual, new_amps)


def solution(mesh):
    return jax.shard_map(
        per_device,
        mesh=mesh,
        in_specs=(
            P("pair", "aux", None),
            P("aux", "pair", None),
            P(),
            P("pair", None, "aux"),
            P(),
            P("pair"),
        ),
        out_specs=(P("pair", None, "aux"), P("pair", None, "aux")),
        check_vma=False,
    )
```

profile of v0, /device:TPU:0, one launch (start us, length us, event | category | flops | bytes accessed | tf_op | source)
XLA Modules:
  0.0 317.7 jit_solution(6276594787825440751)
XLA Ops:
  7.2 0.0 copy-start
  7.2 0.0 all-gather.2.cloned.1.call-start
  7.2 17.7 %all_gather.6 = bf16[1,512,512]{2,1,0:T(8,128)(2,1)} all-gather(bf16[1,64,512]{2,1,0:T(8,128)(2,1)} %param.8), channel_id=1, replica_groups=mesh['pair'=4,'aux'=8] {'aux'}, dimensions={1}, use_global_device_ids=true | all-gather | bytes 589824 | tf_op jit(solution)/shard_map/all_gather | solution.py:25
  25.0 0.0 all-gather.2.cloned.1.call-update
  25.0 0.0 all-reduce.2.cloned.1.call-start
  25.1 4.4 %slice.9 = bf16[512,6,512]{2,1,0:T(8,128)(2,1)} slice(bf16[512,128,512]{2,1,0:T(8,128)(2,1)} %param.9), slice={[0:512], [0:6], [0:512]} | slice | bytes 6291456 | tf_op jit(solution)/shard_map/slice | solution.py:26
  29.4 5.9 %copy_select_fusion = bf16[512,6,512]{2,0,1:T(8,128)(2,1)} fusion(bf16[512,6,512]{2,1,0:T(8,128)(2,1)} %slice.9, pred[]{:T(512)S(6)} %eq.6), kind=kLoop, calls=%fused_computation.7 | loop fusion | flops 1572864 | bytes 6291457 | tf_op jit(solution)/shard_map/jit(_where)/select_n | solution.py:8
  35.4 0.0 all-reduce.2.cloned.1.call-update
  35.4 0.7 slice.12
  36.1 0.2 copy.45
  36.3 0.4 copy-done.1
  36.7 0.5 broadcast.52
  37.2 1.5 reduce.2
  38.7 0.8 reshape.66
  39.5 3.7 %all-to-all-start = ((bf16[4,2,384]{2,1,0:T(2,128)(2,1)}), bf16[4,2,384]{2,1,0:T(2,128)(2,1)S(1)}, u32[]{:S(2)}, u32[]{:S(2)}) async-start(bf16[4,2,384]{2,1,0:T(2,128)(2,1)} %reshape.66), calls=%async_computation | async-start | bytes 12288 | tf_op jit(solution)/shard_map/all_to_all | solution.py:28
  43.2 0.0 reduce-scatter.4.cloned.1.call-start
  43.2 85.2 %copy.44 = bf16[512,128,512]{1,0,2:T(8,128)(2,1)} copy(bf16[512,128,512]{2,1,0:T(8,128)(2,1)} %param.9) | data formatting | bytes 134217728 | tf_op jit(solution)/shard_map/while | solution.py:33
  128.4 0.0 all-to-all-done
  128.4 0.3 reshape.67
  128.7 0.1 copy.46
  128.9 0.0 all-gather.2.cloned.1.call-done
  128.9 22.7 %all-reduce.2.cloned.1.call-done = bf16[512,6,512]{2,0,1:T(8,128)(2,1)} async-done(((bf16[512,6,512]{2,0,1:T(8,128)(2,1)}), bf16[512,6,512]{2,0,1:T(8,128)(2,1)}) %all-reduce.2.cloned.1.call-update) | async-done | bytes 3145744 | tf_op jit(solution)/shard_map/psum | solution.py:9
  151.6 117.1 %while.11 = (s32[]{:T(128)}, f32[4,6,128]{2,0,1:T(4,128)S(1)}, bf16[4,512,512]{2,1,0:T(8,128)(2,1)}, bf16[512,6,512]{2,0,1:T(8,128)(2,1)}, bf16[512,128,512]{1,0,2:T(8,128)(2,1)}) while((s32[]{:T(128)}, f32[4,6,128]{2,0,1:T(4,128)S(1)}, bf16[4,512,512]{2,1,0:T(8,128)(2,1)}, bf16[512,6,512]{2,0,1:T(8,128)(2,1)}, ...), condition=%wide.region_2.3_spmd.clone, body=%wide.region_1.2_spmd.sunk.clone | while | flops 2014838784 | bytes 77085776 | solution.py:33
  151.6 3.9 %convert_bitcast_fusion.3 = bf16[6,512,512]{1,2,0:T(8,128)(2,1)S(1)} fusion(bf16[512,6,512]{2,0,1:T(8,128)(2,1)} %get-tuple-element.128, bf16[4,512,512]{2,1,0:T(8,128)(2,1)} %get-tuple-element.127, s32[]{:T(128)S(6)} %copy.78), kind=kOutput, calls=%fused_computation.2.clone.1.clone | convolution fusion | flops 1612185600 | bytes 6815748 | tf_op jit(solution)/shard_map/while/body/eval_jaxpr/qac,cd->aqd/dot_general | solution.py:13
  155.5 25.3 %fusion.27 = f32[1,6,128]{2,1,0:T(8,128)S(1)} fusion(bf16[512,128,512]{1,0,2:T(8,128)(2,1)} %get-tuple-element.129, bf16[6,512,512]{1,2,0:T(8,128)(2,1)S(1)} %convert_bitcast_fusion.3), kind=kOutput, calls=%fused_computation.3.clone.1.clone | convolution fusion | flops 402653184 | bytes 70257664 | tf_op jit(solution)/shard_map/while/body/eval_jaxpr/aqd,qbd->ab/dot_general | solution.py:19
  180.8 3.9 %convert_bitcast_fusion.3 = bf16[6,512,512]{1,2,0:T(8,128)(2,1)S(1)} fusion(bf16[512,6,512]{2,0,1:T(8,128)(2,1)} %get-tuple-element.128, bf16[4,512,512]{2,1,0:T(8,128)(2,1)} %get-tuple-element.127, s32[]{:T(128)S(6)} %copy.78), kind=kOutput, calls=%fused_computation.2.clone.1.clone | convolution fusion | flops 1612185600 | bytes 6815748 | tf_op jit(solution)/shard_map/while/body/eval_jaxpr/qac,cd->aqd/dot_general | solution.py:13
  184.7 25.3 %fusion.27 = f32[1,6,128]{2,1,0:T(8,128)S(1)} fusion(bf16[512,128,512]{1,0,2:T(8,128)(2,1)} %get-tuple-element.129, bf16[6,512,512]{1,2,0:T(8,128)(2,1)S(1)} %convert_bitcast_fusion.3), kind=kOutput, calls=%fused_computation.3.clone.1.clone | convolution fusion | flops 402653184 | bytes 70257664 | tf_op jit(solution)/shard_map/while/body/eval_jaxpr/aqd,qbd->ab/dot_general | solution.py:19
  210.1 3.9 %convert_bitcast_fusion.3 = bf16[6,512,512]{1,2,0:T(8,128)(2,1)S(1)} fusion(bf16[512,6,512]{2,0,1:T(8,128)(2,1)} %get-tuple-element.128, bf16[4,512,512]{2,1,0:T(8,128)(2,1)} %get-tuple-element.127, s32[]{:T(128)S(6)} %copy.78), kind=kOutput, calls=%fused_computation.2.clone.1.clone | convolution fusion | flops 1612185600 | bytes 6815748 | tf_op jit(solution)/shard_map/while/body/eval_jaxpr/qac,cd->aqd/dot_general | solution.py:13
  214.0 25.3 %fusion.27 = f32[1,6,128]{2,1,0:T(8,128)S(1)} fusion(bf16[512,128,512]{1,0,2:T(8,128)(2,1)} %get-tuple-element.129, bf16[6,512,512]{1,2,0:T(8,128)(2,1)S(1)} %convert_bitcast_fusion.3), kind=kOutput, calls=%fused_computation.3.clone.1.clone | convolution fusion | flops 402653184 | bytes 70257664 | tf_op jit(solution)/shard_map/while/body/eval_jaxpr/aqd,qbd->ab/dot_general | solution.py:19
  239.3 3.9 %convert_bitcast_fusion.3 = bf16[6,512,512]{1,2,0:T(8,128)(2,1)S(1)} fusion(bf16[512,6,512]{2,0,1:T(8,128)(2,1)} %get-tuple-element.128, bf16[4,512,512]{2,1,0:T(8,128)(2,1)} %get-tuple-element.127, s32[]{:T(128)S(6)} %copy.78), kind=kOutput, calls=%fused_computation.2.clone.1.clone | convolution fusion | flops 1612185600 | bytes 6815748 | tf_op jit(solution)/shard_map/while/body/eval_jaxpr/qac,cd->aqd/dot_general | solution.py:13
  243.3 25.3 %fusion.27 = f32[1,6,128]{2,1,0:T(8,128)S(1)} fusion(bf16[512,128,512]{1,0,2:T(8,128)(2,1)} %get-tuple-element.129, bf16[6,512,512]{1,2,0:T(8,128)(2,1)S(1)} %convert_bitcast_fusion.3), kind=kOutput, calls=%fused_computation.3.clone.1.clone | convolution fusion | flops 402653184 | bytes 70257664 | tf_op jit(solution)/shard_map/while/body/eval_jaxpr/aqd,qbd->ab/dot_general | solution.py:19
  268.6 0.0 copy-start.3
  268.6 0.0 copy-start.2
  268.6 0.0 slice-start
  268.6 0.0 copy-done
  268.7 0.1 fusion.8
  268.8 7.2 %all_to_all.36 = f32[4,6,128]{2,1,0:T(8,128)S(1)} all-to-all(f32[4,6,128]{2,1,0:T(8,128)S(1)} %copy.48), channel_id=1, replica_groups=mesh['pair'=4,'aux'=8] {'pair'}, dimensions={0} | all-to-all | bytes 24576 | tf_op jit(solution)/shard_map/all_to_all | solution.py:39
  276.1 0.8 copy.54
  276.8 1.3 bitcast_reduce_fusion
  278.2 0.0 reduce-scatter.4.cloned.1.call-update
  278.8 0.0 copy-done.3
  278.8 0.1 dynamic_slice.11
  278.9 29.3 %reduce-scatter.4.cloned.1.call-done = f32[64,6]{1,0:T(8,128)} async-done(((f32[512,6]{1,0:T(8,128)}), f32[64,6]{1,0:T(8,128)}) %reduce-scatter.4.cloned.1.call-update) | async-done | bytes 1552
  308.2 0.9 reshape_bitcast_fusion
  309.1 0.1 copy.51
  309.3 0.8 divide_subtract_fusion
  310.0 0.6 copy.52
  310.6 0.6 copy.53
  (15 shorter events, 0.2 us)
Async XLA Ops:
  7.2 261.5 %copy-start = (f32[4,4]{1,0:T(4,128)S(1)}, f32[4,4]{1,0:T(4,128)}, u32[]{:S(2)}) copy-start(f32[4,4]{1,0:T(4,128)} %param.10) | copy-start | bytes 196
  7.2 121.7 %all-gather.2.cloned.1.call-start = ((), (), s32[]{:S(2)}) async-start(), calls=%async_computation.3 | async-start | bytes 2621440 | tf_op jit(solution)/shard_map/all_gather | solution.py:33
  25.0 126.6 %all-reduce.2.cloned.1.call-start = ((), (), s32[]{:S(2)}) async-start(), calls=%async_computation.4 | async-start | bytes 6291456 | tf_op jit(solution)/shard_map/psum | solution.py:9
  36.1 0.6 copy-start.1
  39.5 88.9 %all-to-all-start = ((bf16[4,2,384]{2,1,0:T(2,128)(2,1)}), bf16[4,2,384]{2,1,0:T(2,128)(2,1)S(1)}, u32[]{:S(2)}, u32[]{:S(2)}) async-start(bf16[4,2,384]{2,1,0:T(2,128)(2,1)} %reshape.66), calls=%async_computation | async-start | bytes 12288 | tf_op jit(solution)/shard_map/all_to_all | solution.py:28
  43.2 265.0 %reduce-scatter.4.cloned.1.call-start = ((), (), s32[]{:S(2)}) async-start(), calls=%async_computation.5 | async-start | bytes 294912
  268.6 10.2 %copy-start.3 = (f32[512]{0:T(512)S(1)}, f32[512]{0:T(512)}, u32[]{:S(2)}) copy-start(f32[512]{0:T(512)} %param.12) | copy-start | bytes 6148
  268.6 40.7 %copy-start.2 = (f32[1,6,64]{2,0,1:T(1,128)S(1)}, f32[1,6,64]{2,0,1:T(1,128)}, u32[]{:S(2)}) copy-start(f32[1,6,64]{2,0,1:T(1,128)} %param.11) | copy-start | bytes 4612
  268.6 40.6 %slice-start = ((f32[512]{0:T(512)}), f32[6]{0:T(128)S(1)}, s32[]{:S(2)}) async-start(f32[512]{0:T(512)} %param.12), calls=%async_computation.6 | async-start | bytes 1024 | tf_op jit(solution)/shard_map/slice | solution.py:46
Sparse Core Ops, SparseCore 0:
  25.1 36.3 all-gather.1
  64.6 86.9 all-reduce.1
  278.3 29.8 reduce-scatter.3
where the time goes:
time: 320 us; the launch traced here: 318 us
  matrix products  117 us (37%)
  local copies, waits for them, and re-layouts  97.2 us (30%)
  waiting for transfers between devices  52.1 us (16%)
  blocking collectives  25 us (8%)
  between operations  14.5 us (5%)
  other arithmetic  8.19 us (3%)
  starting transfers between devices  3.8 us (1%)
    dot_general x4, matrix products, contract(): jnp.einsum('aqd,qbd->ab', halves, factors, preferred_element_type=jnp.flo...  101 us
    while x1, local copies, waits for them, and re-layouts, per_device(): lax.map(ladder_pair, lax.all_gather(amp_full, 'pair', axis=0, tiled=True))  85.2 us
    unnamed x4, waiting for transfers between devices  29.4 us
    psum x1, waiting for transfers between devices, broadcast(): return lax.psum(block, axis)  22.7 us
    all_gather x1, blocking collectives, per_device(): amp_full = lax.all_gather(amplitudes, 'aux', axis=1, tiled=True)  17.7 us
    dot_general x4, matrix products, half_of(): jnp.einsum('qac,cd->aqd', window, amp_pair, preferred_element_type=jnp.fl...  15.7 us
    all_to_all x1, blocking collectives, per_device(): lax.all_to_all(partial_value, 'pair', split_axis=0, concat_axis=2, tiled=...  7.25 us
  transfers between devices with their start and end apart: 4, of which 2 were waited for; matrix products, arithmetic and copies ran while one was open for 31% of the time, Pallas kernels for 0%

commit v1 on v0

v1 whole, which is shorter than its diff:
```python
import functools

import jax
import jax.numpy as jnp
from jax import lax
from jax.experimental import pallas as pl
from jax.experimental.pallas import tpu as pltpu
from jax.sharding import PartitionSpec as P

MESH = pl.DeviceIdType.MESH
F32 = jnp.float32
BF16 = jnp.bfloat16


def ring_order(n):
    side = 1
    while side * side < n:
        side += 1
    if side * side != n or side % 2:
        return list(range(n))
    order = []
    for row in range(side):
        cols = list(range(1, side))
        if row % 2:
            cols.reverse()
        if row == 0:
            cols = [0] + cols
        order += [row * side + col for col in cols]
    order += [row * side for row in range(side - 1, 0, -1)]
    return order


def lookup(index, table):
    value = jnp.int32(table[0])
    for at, entry in enumerate(table[1:], 1):
        value = jnp.where(index == at, jnp.int32(entry), value)
    return value


def kernel(
    n_pair, n_aux, rows, chunk, slots,
    amp_ref, win_ref, fac_ref,
    sum_ref, slab_ref,
    t_ref, w_ref, f_ref, h_ref, e_ref, part_ref, got_ref,
    f_sem, loc_sem, wl_sem, a_send, a_recv, z_send, z_recv, c_send, c_recv, w_send, w_recv, r_send, r_recv,
):
    width = amp_ref.shape[2]
    own_rows = amp_ref.shape[1]
    block = fac_ref.shape[1]
    chunks = w_ref.shape[0]
    pad = 8
    m = n_aux // 2
    i = lax.axis_index("pair")
    j = lax.axis_index("aux")
    z = j // 2
    core = lax.rem(j, 2)

    order = ring_order(n_pair)
    where = [order.index(k) for k in range(n_pair)]
    pos = lookup(i, where)
    right = lookup(i, [order[(where[k] + 1) % n_pair] for k in range(n_pair)])
    left = lookup(i, [order[(where[k] - 1) % n_pair] for k in range(n_pair)])

    def rows_of(at):
        return pl.ds(pl.multiple_of(at * own_rows, own_rows), own_rows)

    def load_factors(k):
        slot = lax.rem(k, slots)
        return pltpu.make_async_copy(
            fac_ref.at[pl.ds(pl.multiple_of(k * chunk, chunk), chunk)], f_ref.at[slot], f_sem.at[slot]
        )

    local = pltpu.make_async_copy(amp_ref.at[0], t_ref.at[i, rows_of(j)], loc_sem)
    local.start()

    def a_copy(peer, source):
        return pltpu.make_async_remote_copy(
            src_ref=amp_ref.at[0], dst_ref=t_ref.at[source, rows_of(j)],
            send_sem=a_send.at[peer], recv_sem=a_recv.at[source],
            device_id=(peer, j), device_id_type=MESH,
        )

    for step in range(1, n_pair):
        peer = lax.rem(i + step, n_pair)
        a_copy(peer, i).start()

    def w_load(k):
        return pltpu.make_async_copy(win_ref.at[k], w_ref.at[k], wl_sem.at[k])

    def w_copy(k, target):
        return pltpu.make_async_remote_copy(
            src_ref=w_ref.at[k], dst_ref=w_ref.at[k],
            send_sem=w_send.at[k], recv_sem=w_recv.at[k],
            device_id=(target, j), device_id_type=MESH,
        )

    def target_of(k):
        return jnp.where(lax.rem(k, 2) == 0, right, left)

    def distance(k):
        return jnp.where(lax.rem(k, 2) == 0, pos, lax.rem(n_pair - pos, n_pair))

    @pl.when(pos == 0)
    def _():
        @pl.loop(0, chunks)
        def _(k):
            w_load(k).start()

        @pl.loop(0, chunks)
        def _(k):
            w_load(k).wait()
            w_copy(k, target_of(k)).start()

    for k in range(slots):
        load_factors(k).start()

    e_row = lax.broadcasted_iota(jnp.int32, e_ref.shape, 0)
    e_col = lax.broadcasted_iota(jnp.int32, e_ref.shape, 1)
    hit = (e_col == (e_row // pad) * rows + e_row % pad) & (e_row % pad < rows)
    e_ref[...] = jnp.where(hit, 1.0, 0.0).astype(BF16)

    local.wait()
    for step in range(1, n_pair):
        source = lax.rem(i + n_pair - step, n_pair)
        a_copy(i, source).wait_recv()

    def z_copy(peer, source):
        return pltpu.make_async_remote_copy(
            src_ref=t_ref.at[:, rows_of(j)], dst_ref=t_ref.at[:, rows_of(source * 2 + core)],
            send_sem=z_send.at[peer], recv_sem=z_recv.at[source],
            device_id=(i, peer * 2 + core), device_id_type=MESH,
        )

    def c_copy(source, own):
        held = rows_of(source * 2 + own)
        return pltpu.make_async_remote_copy(
            src_ref=t_ref.at[:, held], dst_ref=t_ref.at[:, held],
            send_sem=c_send.at[source], recv_sem=c_recv.at[source],
            device_id=(i, z * 2 + 1 - core), device_id_type=MESH,
        )

    for step in range(1, m):
        z_copy(lax.rem(z + step, m), z).start()
    c_copy(z, core).start()
    for step in range(1, m):
        source = lax.rem(z + m - step, m)
        z_copy(z, source).wait_recv()
        c_copy(source, core).start()

    def handle(k):
        dist = distance(k)
        w_copy(k, target_of(k)).wait_recv()

        @pl.when(dist < n_pair - 1)
        def _():
            w_copy(k, target_of(k)).start()

    def look(k):
        return 2 * (n_pair - 1 - distance(k))

    @pl.when(pos > 0)
    def _():
        @pl.loop(0, chunks)
        def _(k):
            @pl.when(k < look(k))
            def _():
                handle(k)

    for source in range(m):
        c_copy(source, 1 - core).wait_recv()

    part_ref[...] = jnp.zeros_like(part_ref)

    @pl.loop(0, chunks)
    def _(k):
        ahead = k + look(k)

        @pl.when((pos > 0) & (ahead < chunks))
        def _():
            handle(ahead)

        wide = jnp.dot(e_ref[...], w_ref[k], preferred_element_type=F32).astype(BF16)
        for p in range(0, n_pair, 2):
            two = [
                jnp.dot(wide, t_ref[p + at], preferred_element_type=F32).reshape(chunk, pad, width)
                for at in range(2)
            ]
            h_ref[:, p * pad : (p + 2) * pad, :] = jnp.concatenate(two, axis=1).astype(BF16)
        load_factors(k).wait()
        slot = lax.rem(k, slots)

        def add(q, total):
            return total + lax.dot_general(
                f_ref[slot, q], h_ref[q], (((1,), (1,)), ((), ())), preferred_element_type=F32
            )

        total = lax.fori_loop(0, chunk, add, jnp.zeros((block, n_pair * pad), F32), unroll=8)
        part_ref[...] += total.T.reshape(n_pair, pad, block)

        @pl.when(k + slots < chunks)
        def _():
            load_factors(k + slots).start()

    ratio = n_aux // n_pair

    def r_copy(p, t, source, to):
        return pltpu.make_async_remote_copy(
            src_ref=part_ref.at[p], dst_ref=got_ref.at[source],
            send_sem=r_send.at[p * ratio + t], recv_sem=r_recv.at[source],
            device_id=to, device_id_type=MESH,
        )

    for p in range(n_pair):
        for t in range(ratio):
            column = i * ratio + t
            mine = (i == p) & (j == column)

            @pl.when(mine)
            def _():
                got_ref[j] = part_ref[p]

            @pl.when(jnp.logical_not(mine))
            def _():
                r_copy(p, t, j, (jnp.int32(p), column)).start()

    slab_ref[...] = t_ref[:, 0:16, :]
    column_owner = j // ratio
    for source in range(n_aux):
        @pl.when(jnp.logical_not((column_owner == i) & (j == source)))
        def _():
            r_copy(0, 0, source, (i, j)).wait_recv()

    total = got_ref[0]
    for source in range(1, n_aux):
        total = total + got_ref[source]
    sum_ref[...] = total

    for p in range(n_pair):
        for t in range(ratio):
            column = i * ratio + t

            @pl.when(jnp.logical_not((i == p) & (j == column)))
            def _():
                r_copy(p, t, j, (jnp.int32(p), column)).wait_send()
    for step in range(1, n_pair):
        a_copy(lax.rem(i + step, n_pair), i).wait_send()
    for step in range(1, m):
        z_copy(lax.rem(z + step, m), z).wait_send()
    for source in range(m):
        c_copy(source, core).wait_send()

    @pl.loop(0, chunks)
    def _(k):
        @pl.when(distance(k) < n_pair - 1)
        def _():
            w_copy(k, target_of(k)).wait_send()


def per_device(n_pair, n_aux, amplitudes, factors, hole_weights, driver, eps_vir, pair_energy):
    rows, columns = driver.shape[1:]
    depth, block, width = factors.shape
    own_rows = amplitudes.shape[1]
    chunk = min(32, depth)
    chunks = depth // chunk
    slots = min(8, chunks)
    window = factors[:, :rows, :].reshape(chunks, chunk * rows, width)
    pad = 8
    m = n_aux // 2
    ratio = n_aux // n_pair
    vmem = pl.BlockSpec(memory_space=pltpu.VMEM)
    hbm = pl.BlockSpec(memory_space=pl.ANY)
    dma = pltpu.SemaphoreType.DMA
    summed, slab = pl.pallas_call(
        functools.partial(kernel, n_pair, n_aux, rows, chunk, slots),
        out_shape=(
            jax.ShapeDtypeStruct((pad, block), F32),
            jax.ShapeDtypeStruct((n_pair, 16, width), BF16),
        ),
        in_specs=[hbm, hbm, hbm],
        out_specs=(vmem, vmem),
        scratch_shapes=[
            pltpu.VMEM((n_pair, n_aux * own_rows, width), BF16),
            pltpu.VMEM((chunks, chunk * rows, width), BF16),
            pltpu.VMEM((slots, chunk, block, width), BF16),
            pltpu.VMEM((chunk, n_pair * pad, width), BF16),
            pltpu.VMEM((chunk * pad, chunk * rows), BF16),
            pltpu.VMEM((n_pair, pad, block), F32),
            pltpu.VMEM((n_aux, pad, block), F32),
            dma((slots,)),
            dma,
            dma((chunks,)),
            dma((n_pair,)),
            dma((n_pair,)),
            dma((m,)),
            dma((m,)),
            dma((m,)),
            dma((m,)),
            dma((chunks,)),
            dma((chunks,)),
            dma((n_pair * ratio,)),
            dma((n_aux,)),
        ],
        compiler_params=pltpu.CompilerParams(has_side_effects=True, vmem_limit_bytes=60 * 1024 * 1024),
    )(amplitudes, window, factors)

    pair_index = lax.axis_index("pair")
    aux_index = lax.axis_index("aux")
    start = aux_index * columns
    slab_cols = lax.dynamic_slice_in_dim(slab[:, :rows], start, columns, 2).astype(F32)
    weights = lax.dynamic_slice_in_dim(hole_weights, pair_index, 1, 0)[0]
    hole = weights[0] * slab_cols[0]
    for k in range(1, n_pair):
        hole = hole + weights[k] * slab_cols[k]
    particle = lax.dynamic_slice_in_dim(summed[:rows], lax.rem(aux_index, ratio) * columns, columns, 1)
    residual = driver + (particle + hole)[None]
    amp_cols = lax.dynamic_slice_in_dim(slab_cols, pair_index, 1, 0)
    eps_cols = lax.dynamic_slice_in_dim(eps_vir, start, columns, 0)
    denominator = eps_vir[:rows][None, :, None] + eps_cols[None, None, :] - pair_energy[:, None, None]
    return residual, amp_cols - residual / denominator


def solution(mesh):
    return jax.shard_map(
        functools.partial(per_device, mesh.shape["pair"], mesh.shape["aux"]),
        mesh=mesh,
        in_specs=(
            P("pair", "aux", None),
            P("aux", "pair", None),
            P(),
            P("pair", None, "aux"),
            P(),
            P("pair"),
        ),
        out_specs=(P("pair", None, "aux"), P("pair", None, "aux")),
        check_vma=False,
    )
```

time: 320 us -> 116 us (0.36)
  the two profiles are of different devices: /device:TPU:0 before, /device:TPU:13 now
where the time goes in v1:
time: 116 us
  Pallas kernels  97.4 us (84%)
  local copies, waits for them, and re-layouts  13.5 us (12%)
  other arithmetic  3.34 us (3%)
  between operations  1.31 us (1%)
    pallas_call x1, Pallas kernels, per_device(): pl.pallas_call(functools.partial(kernel, n_pair, n_aux, rows, chunk, slot...  97.4 us
    reshape x1, local copies, waits for them, and re-layouts, per_device(): window = factors[:, :rows, :].reshape(chunks, chunk * rows, width)  6.4 us
    slice x1, local copies, waits for them, and re-layouts, per_device(): window = factors[:, :rows, :].reshape(chunks, chunk * rows, width)  4.4 us
    sub x1, other arithmetic, per_device(): return (residual, amp_cols - residual / denominator)  3.26 us

profile of v1, /device:TPU:13, one launch (start us, length us, event | category | flops | bytes accessed | tf_op | source)
XLA Modules:
  0.0 115.5 jit_solution(12586330009218189944)
XLA Ops:
  0.6 0.0 copy-start
  0.6 4.4 %slice.40 = bf16[512,6,512]{2,1,0:T(8,128)(2,1)} slice(bf16[512,128,512]{2,1,0:T(8,128)(2,1)} %fac_ref.1), slice={[0:512], [0:6], [0:512]} | slice | bytes 6291456 | tf_op jit(solution)/shard_map/slice | solution.py:266
  5.0 6.4 %reshape.81.win_ref = bf16[16,192,512]{2,1,0:T(8,128)(2,1)} reshape(bf16[512,6,512]{2,1,0:T(8,128)(2,1)} %slice.40) | data formatting | bytes 6291456 | tf_op jit(solution)/shard_map/reshape | solution.py:266
  11.5 0.0 copy-start.2
  11.5 0.0 copy-start.1
  11.5 0.0 slice-start
  11.5 97.4 %shard_map.77 = (f32[8,128]{1,0:T(8,128)}, bf16[4,16,512]{2,1,0:T(8,128)(2,1)}) custom-call(bf16[1,64,512]{2,1,0:T(8,128)(2,1)} %amp_ref.1, bf16[16,192,512]{2,1,0:T(8,128)(2,1)} %reshape.81.win_ref, bf16[512,128,512]{2,1,0:T(8,128)(2,1)} %fac_ref.1), custom_call_target="tpu_custom_call" | custom-call | tf_op jit(solution)/shard_map/pallas_call | solution.py:273
  108.8 0.8 slice.43
  109.6 0.1 dynamic-slice_convert_fusion
  110.3 0.0 copy-done.2
  110.3 0.1 dynamic_slice.19
  110.4 0.0 copy-done
  110.4 0.7 fusion.8
  111.1 0.0 copy-done.1
  111.1 0.0 slice-done
  111.1 3.3 %divide_subtract_fusion = (f32[1,6,64]{2,1,0:T(8,128)S(1)}, f32[1,6,64]{2,1,0:T(8,128)S(1)}) fusion(f32[4,6,64]{2,1,0:T(8,128)S(1)} %dynamic-slice_convert_fusion, s32[]{:T(128)S(6)} %select_n.12, f32[]{:T(128)} %bitcast.20, f32[64]{0:T(128)S(1)} %dynamic_slice.19, f32[6]{0:T(128)S(1)} %slice-done, f32[]{:T(128)} %bitcast.3, f32[]{:T(128)} %bitcast.2, ...), kind=kLoop, calls=%fused_computation.12 | loop fusion | flops 4992 | bytes 14132 | tf_op jit(solution)/shard_map/sub | solution.py:319
  114.4 0.6 copy.12
  114.9 0.6 copy.13
  (1 shorter events, 0.0 us)
Async XLA Ops:
  0.6 109.8 %copy-start = (f32[4,4]{1,0:T(4,128)S(1)}, f32[4,4]{1,0:T(4,128)}, u32[]{:S(2)}) copy-start(f32[4,4]{1,0:T(4,128)} %param.8) | copy-start | bytes 196
  11.5 98.9 %copy-start.2 = (f32[512]{0:T(512)S(1)}, f32[512]{0:T(512)}, u32[]{:S(2)}) copy-start(f32[512]{0:T(512)} %param.10) | copy-start | bytes 6148
  11.5 99.6 %copy-start.1 = (f32[1,6,64]{2,0,1:T(1,128)S(1)}, f32[1,6,64]{2,0,1:T(1,128)}, u32[]{:S(2)}) copy-start(f32[1,6,64]{2,0,1:T(1,128)} %param.9) | copy-start | bytes 4612
  11.5 99.6 %slice-start = ((f32[512]{0:T(512)}), f32[6]{0:T(128)S(1)}, s32[]{:S(2)}) async-start(f32[512]{0:T(512)} %param.10), calls=%async_computation | async-start | bytes 1024 | tf_op jit(solution)/shard_map/slice | solution.py:318
